TPU v7x, 32 devices: a whole 2x2x4 slice. The times are simulated.
32 devices in a mesh: groups: 2 (over y), dom: 4 (over z), ens: 4 (over x, core).
Axes of the slice: x: 2, y: 2, z: 4, core: 2. Of those that a mesh axis runs over, the one named last changes fastest.
Arguments:
- state: float32 [16, 256, 512], P('ens', ('groups', 'dom')), parts along dimension 1, may hold values from -8 to 8, as said below
- coords: float32 [3, 2048], P(None, ('groups', 'dom')), parts along dimension 1, may hold values from -1 to 1
- owner_local: int32 [2048], P(('groups', 'dom')), parts along dimension 0, may hold values from 0 to 31
- counts: int32 [8, 4], P(('groups', 'dom')), parts along dimension 0, may hold values from 32 to 64, as said below
- obs_value: float32 [2048], P(('groups', 'dom')), parts along dimension 0, may hold values from 0.5 to 3.5
- obs_weight: float32 [2048], P(('groups', 'dom')), parts along dimension 0, as said below
Outputs:
- analysis: float32 [16, 256, 512], P('ens', ('groups', 'dom')), parts along dimension 1
There are 2 independent parts, one for each index of `groups`. A program takes and returns all parts, laid end to end along the dimension named above; each array names one. Nothing has to cross between parts.
Inputs may be any that keep to these rules, and one draw needn't show every extreme that they name: `state`: each member is an independent field plus an offset of its own. The sensors of one block are stored in order of owner block: the first counts[d, 0] slots belong to owner block 0, the next counts[d, 1] to block 1, and so on; slots after the last of them are unused. For one owner block, chosen by the draw, every row holds exactly 64. `obs_weight`: Positive.
All inputs are finite; a program needn't handle non-finite values.
Results may differ from a plain program's by a relative error of at most 0.00028.
Values sent between devices are 32-bit elements; how exact they have to be, the bound alone decides.
No kernel may reach another device: no remote copies, remote signals or barrier semaphores. Data moves between devices by JAX's collectives and lax.ppermute only.
A program may use at most 64 MiB of HBM per device.

v0:
```python
import jax
import jax.numpy as jnp
from jax import lax
from jax.sharding import PartitionSpec as P

CAP = 64
NS_ITERS = 8
GLL_POINTS = (
    -1.0,
    -0.8717401485096066,
    -0.5917001814331423,
    -0.2092992179024789,
    0.2092992179024789,
    0.5917001814331423,
    0.8717401485096066,
    1.0,
)
INFLATION = 1.1


def lagrange(position):
    basis_rows = []
    for node_index in range(8):
        product = jnp.ones_like(position)
        for other_node in range(8):
            if other_node != node_index:
                product = (
                    product
                    * (position - GLL_POINTS[other_node])
                    / (GLL_POINTS[node_index] - GLL_POINTS[other_node])
                )
        basis_rows.append(product)
    return jnp.stack(basis_rows, 0)


def node_weights(sensor_coords):
    along_r = lagrange(sensor_coords[0]).T
    along_s = lagrange(sensor_coords[1]).T
    along_t = lagrange(sensor_coords[2]).T
    node_table = along_t[:, :, None, None] * along_s[:, None, :, None] * along_r[:, None, None, :]
    return node_table.reshape(sensor_coords.shape[1], 512)


def analysis_weights(cross_terms, project):
    highest = lax.Precision.HIGHEST
    members = cross_terms.shape[0]
    identity = jnp.eye(members, dtype=jnp.float32)
    system = cross_terms + (members - 1) / INFLATION * identity
    trace_value = jnp.trace(system)
    iterate = system / trace_value
    inverse_root = identity
    for sweep in range(NS_ITERS):
        middle = 0.5 * (3.0 * identity - jnp.dot(inverse_root, iterate, precision=highest))
        iterate = jnp.dot(iterate, middle, precision=highest)
        inverse_root = jnp.dot(middle, inverse_root, precision=highest)
    mean_weights = (
        jnp.dot(inverse_root, jnp.dot(inverse_root, project, precision=highest), precision=highest)
        / trace_value
    )
    transform = inverse_root * jnp.sqrt((members - 1) / trace_value) + mean_weights[:, None]
    return transform - jnp.mean(transform, axis=0, keepdims=True) + 1.0 / members


def on_device(state, coords, owner_local, counts, obs_value, obs_weight):
    highest = lax.Precision.HIGHEST
    local_members, local_elements, node_count = state.shape
    row_counts = counts[0]
    starts = jnp.cumsum(row_counts) - row_counts
    column = jnp.arange(CAP, dtype=jnp.int32)
    in_use = column[None, :] < row_counts[:, None]
    slot_index = jnp.minimum(starts[:, None] + column[None, :], coords.shape[1] - 1)
    tile_coords = coords[:, slot_index]
    tile_owner = owner_local[slot_index][None]
    tile_obs = obs_value[slot_index]
    tile_weight = jnp.where(in_use, obs_weight[slot_index], jnp.zeros_like(tile_obs))
    node_major = state.transpose(2, 0, 1).reshape(node_count, local_members * local_elements)
    element_ids = jnp.arange(local_elements, dtype=jnp.int32)
    sensor_coords = lax.all_to_all(tile_coords, "dom", split_axis=1, concat_axis=1, tiled=True)
    sources = sensor_coords.shape[1]
    item_count = sensor_coords.shape[2]
    node_table = node_weights(sensor_coords.reshape(3, sources * item_count))
    partial_values = jnp.dot(node_table, node_major, precision=highest)
    partial_values = partial_values.reshape(sources * item_count, local_members, local_elements)
    selector = (
        lax.all_to_all(tile_owner, "dom", split_axis=1, concat_axis=1, tiled=True).reshape(
            sources * item_count, 1
        )
        == element_ids[None, :]
    ).astype(jnp.float32)
    chosen = jnp.sum(partial_values * selector[:, None, :], axis=2)
    owner_values = chosen.T.reshape(local_members, sources, item_count)
    member_part = lax.all_to_all(owner_values, "dom", split_axis=1, concat_axis=1, tiled=True)
    all_values = lax.all_gather(member_part, "ens", axis=0, tiled=True)
    members = all_values.shape[0]
    flat_values = all_values.reshape(members, -1)
    mean_value = jnp.mean(flat_values, axis=0)
    anomaly = flat_values - mean_value[None, :]
    weighted = anomaly * tile_weight.reshape(-1)[None, :]
    cross_terms = jnp.dot(weighted, anomaly.T, precision=highest)
    project = jnp.dot(weighted, tile_obs.reshape(-1) - mean_value, precision=highest)
    cross_terms, project = lax.psum((cross_terms, project), "dom")
    mixing = analysis_weights(cross_terms, project)
    grouped = lax.all_to_all(state, "ens", split_axis=1, concat_axis=0, tiled=True)
    member_total = grouped.shape[0]
    mixed = jnp.dot(mixing.T, grouped.reshape(member_total, -1), precision=highest).reshape(
        grouped.shape
    )
    return lax.all_to_all(mixed, "ens", split_axis=0, concat_axis=1, tiled=True)


def solution(mesh):
    return jax.shard_map(
        on_device,
        mesh=mesh,
        in_specs=(
            P("ens", ("groups", "dom"), None),
            P(None, ("groups", "dom")),
            P(("groups", "dom")),
            P(("groups", "dom"), None),
            P(("groups", "dom")),
            P(("groups", "dom")),
        ),
        out_specs=P("ens", ("groups", "dom"), None),
        check_vma=False,
    )
```

profile of v0, /device:TPU:0, one launch (start us, length us, event | category | flops | bytes accessed | tf_op | source)
XLA Modules:
  0.0 76.4 jit_solution(562660524366019711)
XLA Ops:
  0.0 0.7 copy-done.5
  0.7 0.2 reduce-window.8
  1.0 1.9 %gather_fusion.1 = s32[256]{0:T(256)S(1)} fusion(s32[256]{0:T(256)S(1)} %copy-done, s32[1024]{0:T(1024)S(1)} %pad_clamp_fusion), kind=kCustom, calls=%fused_computation.1 | custom fusion | bytes 3072 | tf_op jit(solution)/shard_map/gather | solution.py:73
  3.0 0.7 broadcast_in_dim.5
  3.7 6.3 %all-to-all-start.1 = ((s32[1,4,64]{2,0,1:T(1,128)}), s32[1,4,64]{2,0,1:T(1,128)S(1)}, u32[]{:S(2)}, u32[]{:S(2)}) async-start(s32[1,4,64]{2,0,1:T(1,128)} %broadcast_in_dim.5), calls=%async_computation.1 | async-start | bytes 4096 | tf_op jit(solution)/shard_map/all_to_all | solution.py:85
  10.2 0.7 gather_fusion
  11.0 0.7 reshape.2397
  11.7 1.9 %gather_fusion.2 = f32[256]{0:T(256)S(1)} fusion(f32[256]{0:T(256)S(1)} %copy-done.1, s32[1024]{0:T(1024)S(1)} %pad_clamp_fusion), kind=kCustom, calls=%fused_computation.2 | custom fusion | bytes 3072 | tf_op jit(solution)/shard_map/gather | solution.py:75
  13.7 1.7 %all-to-all-done.1 = s32[1,4,64]{2,0,1:T(1,128)S(1)} async-done(((s32[1,4,64]{2,0,1:T(1,128)}), s32[1,4,64]{2,0,1:T(1,128)S(1)}, u32[]{:S(2)}, u32[]{:S(2)}) %all-to-all-start.1) | async-done | bytes 1056 | tf_op jit(solution)/shard_map/all_to_all | solution.py:85
  15.4 3.4 %all-to-all-start = ((f32[4,1,192]{2,1,0:T(1,128)}), f32[4,1,192]{2,1,0:T(1,128)S(1)}, u32[]{:S(2)}, u32[]{:S(2)}) async-start(f32[4,1,192]{2,1,0:T(1,128)} %reshape.2397), calls=%async_computation | async-start | bytes 8192 | tf_op jit(solution)/shard_map/all_to_all | solution.py:78
  18.8 0.6 broadcast.3262
  19.4 0.7 reduce.4
  20.2 4.2 %all-to-all-done = f32[4,1,192]{2,1,0:T(1,128)S(1)} async-done(((f32[4,1,192]{2,1,0:T(1,128)}), f32[4,1,192]{2,1,0:T(1,128)S(1)}, u32[]{:S(2)}, u32[]{:S(2)}) %all-to-all-start) | async-done | bytes 3104 | tf_op jit(solution)/shard_map/all_to_all | solution.py:78
  24.4 0.5 broadcast.3265
  24.9 0.6 reduce.5
  27.8 0.9 %copy-done.3 = f32[4,32,512]{2,1,0:T(8,128)S(1)} copy-done((f32[4,32,512]{2,1,0:T(8,128)S(1)}, f32[4,32,512]{2,1,0:T(8,128)}, u32[]{:S(2)}) %copy-start.3) | copy-done | bytes 262168
  28.7 0.5 fusion
  29.2 0.7 reshape.2399
  29.9 3.2 %all-to-all-start.2 = ((f32[4,1,256]{2,1,0:T(1,128)}), f32[4,1,256]{2,1,0:T(1,128)S(1)}, u32[]{:S(2)}, u32[]{:S(2)}) async-start(f32[4,1,256]{2,1,0:T(1,128)} %reshape.2399), calls=%async_computation.2 | async-start | bytes 8192 | tf_op jit(solution)/shard_map/all_to_all | solution.py:92
  33.2 0.9 %copy.45 = f32[4,32,512]{2,0,1:T(4,128)} copy(f32[4,32,512]{2,1,0:T(8,128)S(1)} %copy-done.3) | data formatting | bytes 524288 | tf_op args[0]
  34.1 1.9 %gather_fusion.3 = f32[256]{0:T(256)S(1)} fusion(f32[256]{0:T(256)S(1)} %copy-done.2, s32[1024]{0:T(1024)S(1)} %pad_clamp_fusion), kind=kCustom, calls=%fused_computation.3 | custom fusion | bytes 3072 | tf_op jit(solution)/shard_map/gather | solution.py:74
  36.1 2.6 %all-to-all-done.2 = f32[4,1,256]{2,1,0:T(1,128)S(1)} async-done(((f32[4,1,256]{2,1,0:T(1,128)}), f32[4,1,256]{2,1,0:T(1,128)S(1)}, u32[]{:S(2)}, u32[]{:S(2)}) %all-to-all-start.2) | async-done | bytes 4128 | tf_op jit(solution)/shard_map/all_to_all | solution.py:92
  38.7 3.4 %all-to-all-start.3 = ((f32[4,32,512]{2,0,1:T(4,128)}), f32[4,32,512]{2,0,1:T(4,128)S(1)}, u32[]{:S(2)}, u32[]{:S(2)}) async-start(f32[4,32,512]{2,0,1:T(4,128)} %copy.45), calls=%async_computation.3 | async-start | bytes 524288 | tf_op jit(solution)/shard_map/all_to_all | solution.py:103
  42.1 0.6 reduce.6
  42.8 6.3 %all_gather.3 = f32[16,4,64]{2,1,0:T(4,128)S(1)} all-gather(f32[4,4,64]{2,1,0:T(4,128)S(1)} %copy.42), channel_id=1, replica_groups=mesh['groups'=2,'dom'=4,'ens'=4] {'ens'}, dimensions={0}, use_global_device_ids=true | all-gather | bytes 20480 | tf_op jit(solution)/shard_map/all_gather | solution.py:93
  49.3 0.2 convolution_bitcast_fusion
  49.5 9.9 %all-reduce = (f32[16,16]{1,0:T(8,128)S(1)}, f32[16]{0:T(128)S(1)}) all-reduce(f32[16,16]{1,0:T(8,128)S(1)} %convolution_bitcast_fusion, f32[16]{0:T(128)S(1)} %convolution_bitcast_fusion.1), channel_id=1, replica_groups=mesh['groups'=2,'dom'=4,'ens'=4] {'dom'}, use_global_device_ids=true, to_apply=%region_3.4 | all-reduce | flops 272 | bytes 2176 | tf_op jit(solution)/shard_map/psum | solution.py:101
  59.4 0.7 select_reduce_fusion
  60.1 0.8 %fusion.8 = f32[16,16]{1,0:T(8,128)S(1)} fusion(f32[16,16]{1,0:T(8,128)S(1)} %get-tuple-element.5, f32[]{:T(128)} %select_reduce_fusion), kind=kOutput, calls=%fused_computation.21 | convolution fusion | flops 51456 | bytes 2052 | tf_op jit(solution)/shard_map/dot_general | solution.py:53
  60.9 0.8 %fusion.28 = f32[16,16]{1,0:T(8,128)S(1)} fusion(f32[16,16]{1,0:T(8,128)S(1)} %fusion.8, f32[16,16]{1,0:T(8,128)S(1)} %get-tuple-element.5, f32[]{:T(128)} %select_reduce_fusion), kind=kOutput, calls=%fused_computation.82 | convolution fusion | flops 50176 | bytes 3076 | tf_op jit(solution)/shard_map/dot_general | solution.py:54
  61.9 0.1 fusion.7
  62.0 0.1 fusion.40
  62.3 0.1 fusion.6
  62.4 0.1 fusion.42
  62.7 0.1 fusion.5
  62.8 0.1 fusion.44
  63.1 0.1 fusion.4
  63.3 0.1 fusion.46
  63.5 0.1 fusion.3
  63.7 0.1 fusion.48
  64.0 0.1 fusion.2
  64.4 0.1 fusion.1
  64.7 0.1 convolution_bitcast_fusion.3
  64.8 0.8 %fusion.9 = f32[16]{0:T(128)S(1)} fusion(f32[16,16]{1,0:T(8,128)S(1)} %fusion.51, f32[16,1]{0,1:T(1,128)S(1)} %convolution_bitcast_fusion.3, f32[]{:T(128)} %select_reduce_fusion), kind=kOutput, calls=%fused_computation.26 | convolution fusion | flops 3088 | bytes 1156 | tf_op jit(solution)/shard_map/dot_general | solution.py:57
  66.6 0.6 fusion.10
  67.2 0.2 copy.49
  67.3 8.4 %all_to_all.48 = f32[16,8,512]{2,1,0:T(8,128)S(1)} all-to-all(f32[16,8,512]{2,1,0:T(8,128)S(1)} %copy.49), channel_id=1, replica_groups=mesh['groups'=2,'dom'=4,'ens'=4] {'ens'}, dimensions={0} | all-to-all | bytes 524288 | tf_op jit(solution)/shard_map/all_to_all | solution.py:108
  75.7 0.7 copy.76
  (79 shorter events, 4.8 us)
Async XLA Ops:
  0.0 1.0 %copy-start = (s32[256]{0:T(256)S(1)}, s32[256]{0:T(256)}, u32[]{:S(2)}) copy-start(s32[256]{0:T(256)} %param.8) | copy-start | bytes 3076
  0.0 0.7 copy-start.5
  3.0 7.0 %copy-start.4 = (f32[3,256]{1,0:T(4,128)S(1)}, f32[3,256]{1,0:T(4,128)}, u32[]{:S(2)}) copy-start(f32[3,256]{1,0:T(4,128)} %param.7) | copy-start | bytes 9220
  3.7 11.8 %all-to-all-start.1 = ((s32[1,4,64]{2,0,1:T(1,128)}), s32[1,4,64]{2,0,1:T(1,128)S(1)}, u32[]{:S(2)}, u32[]{:S(2)}) async-start(s32[1,4,64]{2,0,1:T(1,128)} %broadcast_in_dim.5), calls=%async_computation.1 | async-start | bytes 4096 | tf_op jit(solution)/shard_map/all_to_all | solution.py:85
  11.0 0.7 copy-start.1
  15.4 9.0 %all-to-all-start = ((f32[4,1,192]{2,1,0:T(1,128)}), f32[4,1,192]{2,1,0:T(1,128)S(1)}, u32[]{:S(2)}, u32[]{:S(2)}) async-start(f32[4,1,192]{2,1,0:T(1,128)} %reshape.2397), calls=%async_computation | async-start | bytes 8192 | tf_op jit(solution)/shard_map/all_to_all | solution.py:78
  27.7 1.0 %copy-start.3 = (f32[4,32,512]{2,1,0:T(8,128)S(1)}, f32[4,32,512]{2,1,0:T(8,128)}, u32[]{:S(2)}) copy-start(f32[4,32,512]{2,1,0:T(8,128)} %param.6) | copy-start | bytes 786436
  29.9 8.8 %all-to-all-start.2 = ((f32[4,1,256]{2,1,0:T(1,128)}), f32[4,1,256]{2,1,0:T(1,128)S(1)}, u32[]{:S(2)}, u32[]{:S(2)}) async-start(f32[4,1,256]{2,1,0:T(1,128)} %reshape.2399), calls=%async_computation.2 | async-start | bytes 8192 | tf_op jit(solution)/shard_map/all_to_all | solution.py:92
  33.2 0.9 %copy-start.2 = (f32[256]{0:T(256)S(1)}, f32[256]{0:T(256)}, u32[]{:S(2)}) copy-start(f32[256]{0:T(256)} %param.10) | copy-start | bytes 3076
  38.7 27.8 %all-to-all-start.3 = ((f32[4,32,512]{2,0,1:T(4,128)}), f32[4,32,512]{2,0,1:T(4,128)S(1)}, u32[]{:S(2)}, u32[]{:S(2)}) async-start(f32[4,32,512]{2,0,1:T(4,128)} %copy.45), calls=%async_computation.3 | async-start | bytes 524288 | tf_op jit(solution)/shard_map/all_to_all | solution.py:103
where the time goes:
time: 77 us; the launch traced here: 76.4 us
  blocking collectives  24.7 us (32%)
  starting transfers between devices  16.4 us (21%)
  local copies, waits for them, and re-layouts  16 us (21%)
  waiting for transfers between devices  8.47 us (11%)
  matrix products  6.82 us (9%)
  other arithmetic  3.14 us (4%)
  between operations  0.98 us (1%)
    psum x1, blocking collectives, on_device(): cross_terms, project = lax.psum((cross_terms, project), 'dom')  9.93 us
    all_to_all x1, blocking collectives, on_device(): return lax.all_to_all(mixed, 'ens', split_axis=0, concat_axis=1, tiled=True)  8.39 us
    all_to_all x1, starting transfers between devices, on_device(): lax.all_to_all(tile_owner, 'dom', split_axis=1, concat_axis=1, tiled=True)  6.35 us
    all_gather x1, blocking collectives, on_device(): all_values = lax.all_gather(member_part, 'ens', axis=0, tiled=True)  6.34 us
    all_to_all x1, waiting for transfers between devices, on_device(): lax.all_to_all(tile_coords, 'dom', split_axis=1, concat_axis=1, tiled=True)  4.19 us
    unnamed x21, local copies, waits for them, and re-layouts  4.14 us
    all_to_all x1, starting transfers between devices, on_device(): lax.all_to_all(state, 'ens', split_axis=1, concat_axis=0, tiled=True)  3.41 us
    all_to_all x1, starting transfers between devices, on_device(): lax.all_to_all(tile_coords, 'dom', split_axis=1, concat_axis=1, tiled=True)  3.38 us
  transfers between devices with their start and end apart: 4, of which 3 were waited for; matrix products, arithmetic and copies ran while one was open for 20% of the time, Pallas kernels for 0%

commit v1 on v0

--- a/solution.py
+++ b/solution.py
@@ -2,6 +2,7 @@
 import jax.numpy as jnp
 from jax import lax
 from jax.sharding import PartitionSpec as P
+from jax.lax import all_to_all, axis_size
 
 CAP = 64
 NS_ITERS = 8
@@ -16,6 +17,19 @@
     1.0,
 )
 INFLATION = 1.1
+
+
+def cubes_use(view):
+    low = jnp.concatenate(
+        all_to_all(
+            jnp.stack(jnp.split(view, axis_size("dom"), axis=1)),
+            axis_name="dom",
+            split_axis=0,
+            concat_axis=0,
+        ),
+        axis=1,
+    )
+    return low
 
 
 def lagrange(position):
@@ -89,7 +103,7 @@
     ).astype(jnp.float32)
     chosen = jnp.sum(partial_values * selector[:, None, :], axis=2)
     owner_values = chosen.T.reshape(local_members, sources, item_count)
-    member_part = lax.all_to_all(owner_values, "dom", split_axis=1, concat_axis=1, tiled=True)
+    member_part = cubes_use(owner_values)
     all_values = lax.all_gather(member_part, "ens", axis=0, tiled=True)
     members = all_values.shape[0]
     flat_values = all_values.reshape(members, -1)

time: 77 us -> 77 us (level)
    unnamed x21 -> x19, local copies, waits for them, and re-layouts: 4.14 us -> 4.13 us
where the time goes in v1:
time: 77 us; the launch traced here: 76.4 us
  blocking collectives  24.7 us (32%)
  starting transfers between devices  16.4 us (21%)
  local copies, waits for them, and re-layouts  16 us (21%)
  waiting for transfers between devices  8.47 us (11%)
  matrix products  6.82 us (9%)
  other arithmetic  3.16 us (4%)
  between operations  0.98 us (1%)
    psum x1, blocking collectives, on_device(): cross_terms, project = lax.psum((cross_terms, project), 'dom')  9.93 us
    all_to_all x1, blocking collectives, on_device(): return lax.all_to_all(mixed, 'ens', split_axis=0, concat_axis=1, tiled=True)  8.39 us
    all_to_all x1, starting transfers between devices, on_device(): lax.all_to_all(tile_owner, 'dom', split_axis=1, concat_axis=1, tiled=True)  6.35 us
    all_gather x1, blocking collectives, on_device(): all_values = lax.all_gather(member_part, 'ens', axis=0, tiled=True)  6.33 us
    all_to_all x1, waiting for transfers between devices, on_device(): lax.all_to_all(tile_coords, 'dom', split_axis=1, concat_axis=1, tiled=True)  4.19 us
    unnamed x19, local copies, waits for them, and re-layouts  4.13 us
    all_to_all x1, starting transfers between devices, on_device(): lax.all_to_all(state, 'ens', split_axis=1, concat_axis=0, tiled=True)  3.41 us
    all_to_all x1, starting transfers between devices, on_device(): lax.all_to_all(tile_coords, 'dom', split_axis=1, concat_axis=1, tiled=True)  3.38 us
  transfers between devices with their start and end apart: 4, of which 3 were waited for; matrix products, arithmetic and copies ran while one was open for 20% of the time, Pallas kernels for 0%

profile of v1, /device:TPU:0, one launch (start us, length us, event | category | flops | bytes accessed | tf_op | source)
XLA Modules:
  0.0 76.4 jit_solution(6198394552418331400)
XLA Ops:
  0.0 0.7 copy-done.5
  0.7 0.2 reduce-window.8
  1.0 1.9 %gather_fusion.1 = s32[256]{0:T(256)S(1)} fusion(s32[256]{0:T(256)S(1)} %copy-done, s32[1024]{0:T(1024)S(1)} %pad_clamp_fusion), kind=kCustom, calls=%fused_computation.1 | custom fusion | bytes 3072 | tf_op jit(solution)/shard_map/gather | solution.py:87
  3.0 0.7 broadcast_in_dim.5
  3.7 6.3 %all-to-all-start.1 = ((s32[1,4,64]{2,0,1:T(1,128)}), s32[1,4,64]{2,0,1:T(1,128)S(1)}, u32[]{:S(2)}, u32[]{:S(2)}) async-start(s32[1,4,64]{2,0,1:T(1,128)} %broadcast_in_dim.5), calls=%async_computation.1 | async-start | bytes 4096 | tf_op jit(solution)/shard_map/all_to_all | solution.py:99
  10.2 0.7 gather_fusion
  11.0 0.7 reshape.2406
  11.7 1.9 %gather_fusion.2 = f32[256]{0:T(256)S(1)} fusion(f32[256]{0:T(256)S(1)} %copy-done.1, s32[1024]{0:T(1024)S(1)} %pad_clamp_fusion), kind=kCustom, calls=%fused_computation.2 | custom fusion | bytes 3072 | tf_op jit(solution)/shard_map/gather | solution.py:89
  13.7 1.7 %all-to-all-done.1 = s32[1,4,64]{2,0,1:T(1,128)S(1)} async-done(((s32[1,4,64]{2,0,1:T(1,128)}), s32[1,4,64]{2,0,1:T(1,128)S(1)}, u32[]{:S(2)}, u32[]{:S(2)}) %all-to-all-start.1) | async-done | bytes 1056 | tf_op jit(solution)/shard_map/all_to_all | solution.py:99
  15.4 3.4 %all-to-all-start = ((f32[4,1,192]{2,1,0:T(1,128)}), f32[4,1,192]{2,1,0:T(1,128)S(1)}, u32[]{:S(2)}, u32[]{:S(2)}) async-start(f32[4,1,192]{2,1,0:T(1,128)} %reshape.2406), calls=%async_computation | async-start | bytes 8192 | tf_op jit(solution)/shard_map/all_to_all | solution.py:92
  18.8 0.6 broadcast.3262
  19.4 0.7 reduce.5
  20.2 4.2 %all-to-all-done = f32[4,1,192]{2,1,0:T(1,128)S(1)} async-done(((f32[4,1,192]{2,1,0:T(1,128)}), f32[4,1,192]{2,1,0:T(1,128)S(1)}, u32[]{:S(2)}, u32[]{:S(2)}) %all-to-all-start) | async-done | bytes 3104 | tf_op jit(solution)/shard_map/all_to_all | solution.py:92
  24.4 0.5 broadcast.3263
  24.9 0.6 reduce.6
  27.8 0.9 %copy-done.3 = f32[4,32,512]{2,1,0:T(8,128)S(1)} copy-done((f32[4,32,512]{2,1,0:T(8,128)S(1)}, f32[4,32,512]{2,1,0:T(8,128)}, u32[]{:S(2)}) %copy-start.3) | copy-done | bytes 262168
  28.7 0.5 fusion
  29.2 0.7 reshape.2408
  29.9 3.2 %all-to-all-start.2 = ((f32[4,1,256]{2,1,0:T(1,128)}), f32[4,1,256]{2,1,0:T(1,128)S(1)}, u32[]{:S(2)}, u32[]{:S(2)}) async-start(f32[4,1,256]{2,1,0:T(1,128)} %reshape.2408), calls=%async_computation.2 | async-start | bytes 8192 | tf_op jit(solution)/shard_map/all_to_all | solution.py:24
  33.2 0.9 %copy.53 = f32[4,32,512]{2,0,1:T(4,128)} copy(f32[4,32,512]{2,1,0:T(8,128)S(1)} %copy-done.3) | data formatting | bytes 524288 | tf_op args[0]
  34.1 1.9 %gather_fusion.3 = f32[256]{0:T(256)S(1)} fusion(f32[256]{0:T(256)S(1)} %copy-done.2, s32[1024]{0:T(1024)S(1)} %pad_clamp_fusion), kind=kCustom, calls=%fused_computation.3 | custom fusion | bytes 3072 | tf_op jit(solution)/shard_map/gather | solution.py:88
  36.1 2.6 %all-to-all-done.2 = f32[4,1,256]{2,1,0:T(1,128)S(1)} async-done(((f32[4,1,256]{2,1,0:T(1,128)}), f32[4,1,256]{2,1,0:T(1,128)S(1)}, u32[]{:S(2)}, u32[]{:S(2)}) %all-to-all-start.2) | async-done | bytes 4128 | tf_op jit(solution)/shard_map/all_to_all | solution.py:24
  38.7 3.4 %all-to-all-start.3 = ((f32[4,32,512]{2,0,1:T(4,128)}), f32[4,32,512]{2,0,1:T(4,128)S(1)}, u32[]{:S(2)}, u32[]{:S(2)}) async-start(f32[4,32,512]{2,0,1:T(4,128)} %copy.53), calls=%async_computation.3 | async-start | bytes 524288 | tf_op jit(solution)/shard_map/all_to_all | solution.py:117
  42.1 0.6 reduce.7
  42.8 6.3 %all-gather = f32[16,4,1,64]{3,1,2,0:T(4,128)S(1)} all-gather(f32[4,4,1,64]{3,1,2,0:T(4,128)S(1)} %copy.50), channel_id=2, replica_groups=mesh['groups'=2,'dom'=4,'ens'=4] {'ens'}, dimensions={0}, use_global_device_ids=true | all-gather | bytes 20480 | tf_op jit(solution)/shard_map/all_gather | solution.py:107
  49.3 0.2 convolution_bitcast_fusion
  49.5 9.9 %all-reduce = (f32[16,16]{1,0:T(8,128)S(1)}, f32[16]{0:T(128)S(1)}) all-reduce(f32[16,16]{1,0:T(8,128)S(1)} %convolution_bitcast_fusion, f32[16]{0:T(128)S(1)} %convolution_bitcast_fusion.1), channel_id=1, replica_groups=mesh['groups'=2,'dom'=4,'ens'=4] {'dom'}, use_global_device_ids=true, to_apply=%region_3.4 | all-reduce | flops 272 | bytes 2176 | tf_op jit(solution)/shard_map/psum | solution.py:115
  59.4 0.7 select_reduce_fusion
  60.1 0.8 %fusion.8 = f32[16,16]{1,0:T(8,128)S(1)} fusion(f32[16,16]{1,0:T(8,128)S(1)} %get-tuple-element.5, f32[]{:T(128)} %select_reduce_fusion), kind=kOutput, calls=%fused_computation.21 | convolution fusion | flops 51456 | bytes 2052 | tf_op jit(solution)/shard_map/dot_general | solution.py:67
  60.9 0.8 %fusion.28 = f32[16,16]{1,0:T(8,128)S(1)} fusion(f32[16,16]{1,0:T(8,128)S(1)} %fusion.8, f32[16,16]{1,0:T(8,128)S(1)} %get-tuple-element.5, f32[]{:T(128)} %select_reduce_fusion), kind=kOutput, calls=%fused_computation.83 | convolution fusion | flops 50176 | bytes 3076 | tf_op jit(solution)/shard_map/dot_general | solution.py:68
  61.9 0.1 fusion.7
  62.0 0.1 fusion.42
  62.3 0.1 fusion.6
  62.4 0.1 fusion.44
  62.7 0.1 fusion.5
  62.8 0.1 fusion.46
  63.1 0.1 fusion.4
  63.3 0.1 fusion.48
  63.5 0.1 fusion.3
  63.7 0.1 fusion.50
  64.0 0.1 fusion.2
  64.4 0.1 fusion.1
  64.7 0.1 convolution_bitcast_fusion.3
  64.8 0.8 %fusion.9 = f32[16]{0:T(128)S(1)} fusion(f32[16,16]{1,0:T(8,128)S(1)} %fusion.53, f32[16,1]{0,1:T(1,128)S(1)} %convolution_bitcast_fusion.3, f32[]{:T(128)} %select_reduce_fusion), kind=kOutput, calls=%fused_computation.26 | convolution fusion | flops 3088 | bytes 1156 | tf_op jit(solution)/shard_map/dot_general | solution.py:71
  66.6 0.6 fusion.10
  67.2 0.2 copy.57
  67.3 8.4 %all_to_all.48 = f32[16,8,512]{2,1,0:T(8,128)S(1)} all-to-all(f32[16,8,512]{2,1,0:T(8,128)S(1)} %copy.57), channel_id=1, replica_groups=mesh['groups'=2,'dom'=4,'ens'=4] {'ens'}, dimensions={0} | all-to-all | bytes 524288 | tf_op jit(solution)/shard_map/all_to_all | solution.py:122
  75.7 0.7 copy.86
  (79 shorter events, 4.8 us)
Async XLA Ops:
  0.0 1.0 %copy-start = (s32[256]{0:T(256)S(1)}, s32[256]{0:T(256)}, u32[]{:S(2)}) copy-start(s32[256]{0:T(256)} %param.8) | copy-start | bytes 3076
  0.0 0.7 copy-start.5
  3.0 7.0 %copy-start.4 = (f32[3,256]{1,0:T(4,128)S(1)}, f32[3,256]{1,0:T(4,128)}, u32[]{:S(2)}) copy-start(f32[3,256]{1,0:T(4,128)} %param.7) | copy-start | bytes 9220
  3.7 11.8 %all-to-all-start.1 = ((s32[1,4,64]{2,0,1:T(1,128)}), s32[1,4,64]{2,0,1:T(1,128)S(1)}, u32[]{:S(2)}, u32[]{:S(2)}) async-start(s32[1,4,64]{2,0,1:T(1,128)} %broadcast_in_dim.5), calls=%async_computation.1 | async-start | bytes 4096 | tf_op jit(solution)/shard_map/all_to_all | solution.py:99
  11.0 0.7 copy-start.1
  15.4 9.0 %all-to-all-start = ((f32[4,1,192]{2,1,0:T(1,128)}), f32[4,1,192]{2,1,0:T(1,128)S(1)}, u32[]{:S(2)}, u32[]{:S(2)}) async-start(f32[4,1,192]{2,1,0:T(1,128)} %reshape.2406), calls=%async_computation | async-start | bytes 8192 | tf_op jit(solution)/shard_map/all_to_all | solution.py:92
  27.7 1.0 %copy-start.3 = (f32[4,32,512]{2,1,0:T(8,128)S(1)}, f32[4,32,512]{2,1,0:T(8,128)}, u32[]{:S(2)}) copy-start(f32[4,32,512]{2,1,0:T(8,128)} %param.6) | copy-start | bytes 786436
  29.9 8.8 %all-to-all-start.2 = ((f32[4,1,256]{2,1,0:T(1,128)}), f32[4,1,256]{2,1,0:T(1,128)S(1)}, u32[]{:S(2)}, u32[]{:S(2)}) async-start(f32[4,1,256]{2,1,0:T(1,128)} %reshape.2408), calls=%async_computation.2 | async-start | bytes 8192 | tf_op jit(solution)/shard_map/all_to_all | solution.py:24
  33.2 0.9 %copy-start.2 = (f32[256]{0:T(256)S(1)}, f32[256]{0:T(256)}, u32[]{:S(2)}) copy-start(f32[256]{0:T(256)} %param.10) | copy-start | bytes 3076
  38.7 27.8 %all-to-all-start.3 = ((f32[4,32,512]{2,0,1:T(4,128)}), f32[4,32,512]{2,0,1:T(4,128)S(1)}, u32[]{:S(2)}, u32[]{:S(2)}) async-start(f32[4,32,512]{2,0,1:T(4,128)} %copy.53), calls=%async_computation.3 | async-start | bytes 524288 | tf_op jit(solution)/shard_map/all_to_all | solution.py:117
